TPU v7x, 32 devices: a whole 2x2x4 slice. The times are simulated.
32 devices in a mesh: ctx: 2 (over x), tp: 4 (over z), dp: 4 (over y, core).
Axes of the slice: x: 2, y: 2, z: 4, core: 2. Of those that a mesh axis runs over, the one named last changes fastest.
Arguments:
- queries: bfloat16 [4, 256, 4096], P('dp', 'ctx', 'tp'), may hold values from -6 to 6
- keys: bfloat16 [4, 2, 4, 32, 128, 128], P('dp', None, 'tp', 'ctx'), may hold values from -6 to 6
- values: bfloat16 [4, 2, 4, 32, 128, 128], P('dp', None, 'tp', 'ctx'), may hold values from -6 to 6
- cotangent: bfloat16 [4, 256, 4096], P('dp', 'ctx', 'tp'), may hold values from -6 to 6
- lengths: int32 [4, 4, 2], P('dp'), may hold values from 16 to 128
Outputs:
- attended: bfloat16 [4, 256, 4096], P('dp', 'ctx', 'tp')
- grad_queries: bfloat16 [4, 256, 4096], P('dp', 'ctx', 'tp')
- grad_keys: bfloat16 [4, 2, 4, 32, 128, 128], P('dp', None, 'tp', 'ctx')
- grad_values: bfloat16 [4, 2, 4, 32, 128, 128], P('dp', None, 'tp', 'ctx')
Inputs may be any that keep to these rules, and one draw needn't show every extreme that they name: Neighbour n of span u has its first lengths[u, n] tokens live; the others are padding.
All inputs are finite; a program needn't handle non-finite values.
Results may differ from a plain program's by a relative error of at most 0.012.
The roundings to bfloat16 on the way count: a program that leaves them out, or rounds other values in their place, can miss the bound.
Values may be sent and summed in bfloat16 or wider, within the bound.
A program may use at most 64 MiB of HBM per device.

v0:
```python
import math

import jax
import jax.numpy as jnp
from jax import lax
from jax.sharding import PartitionSpec as P

DH = 128
SPAN = 64
NBR = 2


def from_behind(block, axis, distance):
    devices = range(lax.axis_size(axis))
    route = [(i - distance, i) for i in devices if i - distance in devices]
    return lax.ppermute(block, axis, route)


def rotate(tensor, direction):
    middle = tensor.shape[-1] // 2
    frequency = 10000.0 ** (-2.0 * jnp.arange(middle, dtype=jnp.float32) / tensor.shape[-1])
    angles = jnp.arange(tensor.shape[-2], dtype=jnp.float32)[:, None] * frequency[None, :]
    cosine = jnp.cos(angles)
    sine_part = direction * jnp.sin(angles)
    lower_part = tensor[..., :middle].astype(jnp.float32)
    upper_part = tensor[..., middle:].astype(jnp.float32)
    return jnp.concatenate(
        [
            lower_part * cosine - upper_part * sine_part,
            lower_part * sine_part + upper_part * cosine,
        ],
        axis=-1,
    )


def live_scores(query_rows, key_rows, key_counts):
    scaling = 1.0 / math.sqrt(query_rows.shape[-1])
    scores = (
        jnp.einsum("zhid,zhjd->zhij", query_rows, key_rows, preferred_element_type=jnp.float32)
        * scaling
    )
    usable = lax.broadcasted_iota(jnp.int32, scores.shape, 3) < key_counts[:, None, None, None]
    return jnp.where(usable, scores, -jnp.inf)


def neighbour_forward(query_rows, key_rows, value_rows, key_counts):
    scores = live_scores(query_rows, key_rows, key_counts)
    maxima = jnp.max(scores, axis=-1, keepdims=True)
    weights = jnp.exp(scores - maxima)
    totals = jnp.sum(weights, axis=-1)
    summed = jnp.einsum(
        "zhij,zhjd->zhid",
        weights.astype(jnp.bfloat16),
        value_rows,
        preferred_element_type=jnp.float32,
    )
    return (summed / totals[..., None], maxima[..., 0] + jnp.log(totals))


def neighbour_backward(
    query_rows, key_rows, value_rows, key_counts, grad_rows, log_totals, output_dots
):
    scaling = 1.0 / math.sqrt(query_rows.shape[-1])
    scores = live_scores(query_rows, key_rows, key_counts)
    chances = jnp.exp(scores - log_totals[..., None])
    grad_values = jnp.einsum(
        "zhij,zhid->zhjd",
        chances.astype(jnp.bfloat16),
        grad_rows,
        preferred_element_type=jnp.float32,
    )
    grad_weights = jnp.einsum(
        "zhid,zhjd->zhij", grad_rows, value_rows, preferred_element_type=jnp.float32
    )
    grad_scores = (chances * (grad_weights - output_dots[..., None]) * scaling).astype(jnp.bfloat16)
    grad_query = jnp.einsum(
        "zhij,zhjd->zhid", grad_scores, key_rows, preferred_element_type=jnp.float32
    ).astype(jnp.bfloat16)
    grad_key = jnp.einsum(
        "zhij,zhid->zhjd", grad_scores, query_rows, preferred_element_type=jnp.float32
    )
    return (grad_query, grad_key, grad_values)


def combine_pairs(partial_value, log_parts, blocks):
    partial_value = partial_value.reshape((blocks, NBR) + partial_value.shape[1:])
    log_parts = log_parts.reshape((blocks, NBR) + log_parts.shape[1:])
    log_whole = jax.nn.logsumexp(log_parts, axis=1)
    attended = jnp.sum(
        jnp.exp(log_parts - log_whole[:, None])[..., None] * partial_value, axis=1
    ).astype(jnp.bfloat16)
    return (attended, log_whole)


def window_of(tokens, tail_rows, blocks, heads_here):
    joined = jnp.concatenate([tokens[0, SPAN - 1 :], tail_rows[0]], axis=0)
    return joined.reshape(blocks, SPAN, heads_here, DH).transpose(0, 2, 1, 3)


def rows_of(window_rows):
    return window_rows.transpose(0, 2, 1, 3).reshape(
        window_rows.shape[0] * window_rows.shape[2], -1
    )


def shards(queries, keys, values, cotangent, lengths):
    rows_dev = queries.shape[1]
    blocks = rows_dev // SPAN
    heads_here = queries.shape[2] // DH
    rim_rows = SPAN - 1
    tail_queries, tail_grads = from_behind(
        (queries[:, :rim_rows], cotangent[:, :rim_rows]), "ctx", -1
    )
    query_turned = rotate(window_of(queries, tail_queries, blocks, heads_here), 1.0).astype(
        jnp.bfloat16
    )
    window_grads = window_of(cotangent, tail_grads, blocks, heads_here)
    position = lax.axis_index("ctx")
    key_rows, value_rows = (
        lax.all_to_all(
            lax.all_to_all(keys, "ctx", split_axis=1, concat_axis=3, tiled=True),
            "tp",
            split_axis=3,
            concat_axis=2,
            tiled=True,
        ),
        lax.all_to_all(
            lax.all_to_all(values, "ctx", split_axis=1, concat_axis=3, tiled=True),
            "tp",
            split_axis=3,
            concat_axis=2,
            tiled=True,
        ),
    )
    key_turned = rotate(key_rows[0, 0], 1.0).astype(jnp.bfloat16)
    value_here = value_rows[0, 0]
    own_counts = lax.dynamic_slice_in_dim(lengths[0], position * blocks, blocks, 0).reshape(-1)
    query_copies = jnp.repeat(query_turned, NBR, axis=0)
    partial_value, log_parts = neighbour_forward(query_copies, key_turned, value_here, own_counts)
    attended, log_whole = combine_pairs(partial_value, log_parts, blocks)
    output_dots = jnp.sum(window_grads.astype(jnp.float32) * attended.astype(jnp.float32), axis=-1)
    grad_query, grad_key, grad_values = neighbour_backward(
        query_copies,
        key_turned,
        value_here,
        own_counts,
        jnp.repeat(window_grads, NBR, axis=0),
        jnp.repeat(log_whole, NBR, axis=0),
        jnp.repeat(output_dots, NBR, axis=0),
    )
    key_back = rotate(grad_key, -1.0).astype(jnp.bfloat16)[None, None]
    value_back = grad_values.astype(jnp.bfloat16)[None, None]
    swapped = (
        lax.all_to_all(key_back, "tp", split_axis=2, concat_axis=3, tiled=True),
        lax.all_to_all(value_back, "tp", split_axis=2, concat_axis=3, tiled=True),
    )
    grad_keys, grad_vals = (
        lax.all_to_all(swapped[0], "ctx", split_axis=3, concat_axis=1, tiled=True),
        lax.all_to_all(swapped[1], "ctx", split_axis=3, concat_axis=1, tiled=True),
    )
    grad_sum = jnp.sum(
        grad_query.reshape(blocks, NBR, heads_here, SPAN, DH).astype(jnp.float32), axis=1
    )
    grad_window = rotate(grad_sum, -1.0).astype(jnp.bfloat16)
    attended_rows = rows_of(attended)
    grad_rows = rows_of(grad_window)
    carried_out = from_behind(attended_rows[rows_dev - rim_rows :], "ctx", 1)
    carried_grad = from_behind(grad_rows[rows_dev - rim_rows :], "ctx", 1)
    attended_tokens = jnp.concatenate([carried_out, attended_rows[: rows_dev - rim_rows]], axis=0)[
        None
    ]
    grad_tokens = jnp.concatenate([carried_grad, grad_rows[: rows_dev - rim_rows]], axis=0)[None]
    return (attended_tokens, grad_tokens, grad_keys, grad_vals)


def solution(mesh):
    in_specs = (
        P("dp", "ctx", "tp"),
        P("dp", None, "tp", "ctx", None, None),
        P("dp", None, "tp", "ctx", None, None),
        P("dp", "ctx", "tp"),
        P("dp", None, None),
    )
    out_specs = (
        P("dp", "ctx", "tp"),
        P("dp", "ctx", "tp"),
        P("dp", None, "tp", "ctx", None, None),
        P("dp", None, "tp", "ctx", None, None),
    )
    return jax.shard_map(shards, mesh=mesh, in_specs=in_specs, out_specs=out_specs, check_vma=False)
```

profile of v0, /device:TPU:24, one launch (start us, length us, event | category | flops | bytes accessed | tf_op | source)
XLA Modules:
  0.0 187.8 jit_solution(7407794268431638645)
XLA Ops:
  0.6 0.0 copy-start
  0.7 18.5 %all_to_all.90 = bf16[1,2,1,16,128,128]{5,4,3,2,0,1:T(8,128)(2,1)} all-to-all(bf16[1,2,1,16,128,128]{5,4,3,2,0,1:T(8,128)(2,1)} %bitcast.116), channel_id=1, replica_groups=mesh['ctx'=2,'tp'=4,'dp'=4] {'ctx'}, dimensions={1} | all-to-all | bytes 2097152 | tf_op jit(solution)/shard_map/all_to_all | solution.py:121
  19.1 4.4 %all-to-all-start.2 = ((bf16[1,2,1,16,128,128]{5,4,3,2,0,1:T(8,128)(2,1)}), bf16[1,2,1,16,128,128]{5,4,3,2,0,1:T(8,128)(2,1)}, u32[]{:S(2)}, u32[]{:S(2)}) async-start(bf16[1,2,1,16,128,128]{5,4,3,2,0,1:T(8,128)(2,1)} %bitcast.9), calls=%async_computation.2 | async-start | bytes 2097152 | tf_op jit(solution)/shard_map/all_to_all | solution.py:128
  23.6 1.3 collective-permute-start.2
  24.9 1.3 collective-permute-start
  26.2 12.4 %all-to-all-done.2 = bf16[1,2,1,16,128,128]{5,4,3,2,0,1:T(8,128)(2,1)} async-done(((bf16[1,2,1,16,128,128]{5,4,3,2,0,1:T(8,128)(2,1)}), bf16[1,2,1,16,128,128]{5,4,3,2,0,1:T(8,128)(2,1)}, u32[]{:S(2)}, u32[]{:S(2)}) %all-to-all-start.2) | async-done | bytes 1048608 | tf_op jit(solution)/shard_map/all_to_all | solution.py:128
  38.7 5.1 %all-to-all-start.1 = ((bf16[1,1,1,32,128,128]{5,4,2,1,0,3:T(8,128)(2,1)}), bf16[1,1,1,32,128,128]{5,4,2,1,0,3:T(8,128)(2,1)S(1)}, u32[]{:S(2)}, u32[]{:S(2)}) async-start(bf16[1,1,1,32,128,128]{5,4,2,1,0,3:T(8,128)(2,1)} %bitcast.6), calls=%async_computation.1 | async-start | bytes 2097152 | tf_op jit(solution)/shard_map/all_to_all | solution.py:120
  43.8 0.9 broadcast_multiply_fusion
  44.8 0.7 broadcast_multiply_fusion.1
  45.5 0.1 constant_dynamic-slice_fusion
  45.6 0.1 copy.29
  45.7 0.1 lt.18
  45.8 0.0 collective-permute-done
  45.9 0.0 collective-permute-done.2
  46.0 0.8 copy.52
  46.7 1.7 copy.62
  48.4 0.2 fusion.15
  48.7 0.2 pad_maximum_fusion.1
  48.9 14.6 %all-to-all-done.1 = bf16[1,1,1,32,128,128]{5,4,2,1,0,3:T(8,128)(2,1)S(1)} async-done(((bf16[1,1,1,32,128,128]{5,4,2,1,0,3:T(8,128)(2,1)}), bf16[1,1,1,32,128,128]{5,4,2,1,0,3:T(8,128)(2,1)S(1)}, u32[]{:S(2)}, u32[]{:S(2)}) %all-to-all-start.1) | async-done | bytes 1048608 | tf_op jit(solution)/shard_map/all_to_all | solution.py:120
  63.4 5.8 %all-to-all-start.3 = ((bf16[1,1,1,32,128,128]{5,4,2,1,0,3:T(8,128)(2,1)}), bf16[1,1,1,32,128,128]{5,4,2,1,0,3:T(8,128)(2,1)S(1)}, u32[]{:S(2)}, u32[]{:S(2)}) async-start(bf16[1,1,1,32,128,128]{5,4,2,1,0,3:T(8,128)(2,1)} %bitcast.11), calls=%async_computation.3 | async-start | bytes 2097152 | tf_op jit(solution)/shard_map/all_to_all | solution.py:127
  69.3 1.7 fusion.1
  71.0 0.0 copy-start.1
  71.0 0.1 broadcast_in_dim.19
  71.1 0.0 copy-start.9
  71.1 1.0 fusion.31
  72.1 0.6 fusion.12
  72.8 0.0 copy-done.7
  72.9 0.1 broadcast_in_dim.23
  73.0 0.0 copy-start.13
  73.0 0.8 copy-done.3
  73.8 2.0 %fusion.4 = bf16[1,1,4,8,128,128]{5,4,3,1,0,2:T(8,128)(2,1)} fusion(bf16[4,8,64,128]{3,2,1,0:T(8,128)(2,1)S(1)} %bitcast.103, f32[4,8,64,128]{3,2,1,0:T(8,128)S(1)} %get-tuple-element.27, f32[4,8,64]{2,1,0:T(8,128)S(1)} %bitcast.120), kind=kOutput, calls=%fused_computation.11 | convolution fusion | flops 68157440 | bytes 2629632 | tf_op jit(solution)/shard_map/zhij,zhid->zhjd/dot_general | solution.py:66
  75.8 15.0 %all-to-all-done.3 = bf16[1,1,1,32,128,128]{5,4,2,1,0,3:T(8,128)(2,1)S(1)} async-done(((bf16[1,1,1,32,128,128]{5,4,2,1,0,3:T(8,128)(2,1)}), bf16[1,1,1,32,128,128]{5,4,2,1,0,3:T(8,128)(2,1)S(1)}, u32[]{:S(2)}, u32[]{:S(2)}) %all-to-all-start.3) | async-done | bytes 1048608 | tf_op jit(solution)/shard_map/all_to_all | solution.py:127
  90.9 6.6 %all-to-all-start.6 = ((bf16[1,1,4,8,128,128]{5,4,3,1,0,2:T(8,128)(2,1)}), bf16[1,1,4,8,128,128]{5,4,3,1,0,2:T(8,128)(2,1)}, u32[]{:S(2)}, u32[]{:S(2)}) async-start(bf16[1,1,4,8,128,128]{5,4,3,1,0,2:T(8,128)(2,1)} %fusion.4), calls=%async_computation.6 | async-start | bytes 2097152 | tf_op jit(solution)/shard_map/all_to_all | solution.py:155
  97.5 1.0 multiply_reduce_fusion
  98.5 0.0 copy-start.8
  98.6 1.2 multiply_reduce_fusion.1
  99.8 0.0 copy-done.4
  99.8 0.0 copy-done.14
  99.8 1.0 fusion.8
  100.8 0.8 copy-done.5
  101.6 0.5 fusion.32
  102.1 0.3 copy-done.12
  102.5 0.8 fusion.9
  103.3 0.6 maximum_bitcast_fusion
  103.9 16.6 %all-to-all-done.6 = bf16[1,1,4,8,128,128]{5,4,3,1,0,2:T(8,128)(2,1)} async-done(((bf16[1,1,4,8,128,128]{5,4,3,1,0,2:T(8,128)(2,1)}), bf16[1,1,4,8,128,128]{5,4,3,1,0,2:T(8,128)(2,1)}, u32[]{:S(2)}, u32[]{:S(2)}) %all-to-all-start.6) | async-done | bytes 1048608 | tf_op jit(solution)/shard_map/all_to_all | solution.py:155
  120.5 28.4 %all_to_all.91 = bf16[1,1,4,8,128,128]{5,4,3,1,0,2:T(8,128)(2,1)} all-to-all(bf16[1,1,4,8,128,128]{5,4,3,1,0,2:T(8,128)(2,1)S(1)} %maximum_bitcast_fusion), channel_id=1, replica_groups=mesh['ctx'=2,'tp'=4,'dp'=4] {'tp'}, dimensions={2} | all-to-all | bytes 2097152 | tf_op jit(solution)/shard_map/all_to_all | solution.py:154
  148.9 4.6 %all-to-all-start.7 = ((bf16[1,1,1,32,128,128]{5,4,2,1,0,3:T(8,128)(2,1)}), bf16[1,1,1,32,128,128]{5,4,2,1,0,3:T(8,128)(2,1)}, u32[]{:S(2)}, u32[]{:S(2)}) async-start(bf16[1,1,1,32,128,128]{5,4,2,1,0,3:T(8,128)(2,1)} %bitcast.35), calls=%async_computation.7 | async-start | bytes 2097152 | tf_op jit(solution)/shard_map/all_to_all | solution.py:159
  153.5 0.2 copy.35
  153.7 0.7 slice.68
  154.4 4.7 %collective-permute-start.1 = (bf16[63,1024]{1,0:T(8,128)(2,1)}, bf16[63,1024]{1,0:T(8,128)(2,1)}, u32[]{:S(2)}, u32[]{:S(2)}) collective-permute-start(bf16[63,1024]{1,0:T(8,128)(2,1)} %slice.68), channel_id=1, source_target_pairs={{0,16},{1,17},{2,18},{3,19},{4,20},{5,21},{6,22},{7,23},{8,24},{9,... | collective-permute-start | bytes 387080 | tf_op jit(solution)/shard_map/ppermute | solution.py:16
  159.1 0.7 convert_reduce_fusion
  159.8 7.2 %all-to-all-done.7 = bf16[1,1,1,32,128,128]{5,4,2,1,0,3:T(8,128)(2,1)} async-done(((bf16[1,1,1,32,128,128]{5,4,2,1,0,3:T(8,128)(2,1)}), bf16[1,1,1,32,128,128]{5,4,2,1,0,3:T(8,128)(2,1)}, u32[]{:S(2)}, u32[]{:S(2)}) %all-to-all-start.7) | async-done | bytes 1048608 | tf_op jit(solution)/shard_map/all_to_all | solution.py:159
  167.0 3.6 %all-to-all-start.5 = ((bf16[1,1,1,32,128,128]{5,4,2,1,0,3:T(8,128)(2,1)}), bf16[1,1,1,32,128,128]{5,4,2,1,0,3:T(8,128)(2,1)S(1)}, u32[]{:S(2)}, u32[]{:S(2)}) async-start(bf16[1,1,1,32,128,128]{5,4,2,1,0,3:T(8,128)(2,1)} %bitcast.107), calls=%async_computation.5 | async-start | bytes 2097152 | tf_op jit(solution)/shard_map/all_to_all | solution.py:158
  170.6 0.3 subtract_convert_fusion.1
  170.9 0.2 maximum_bitcast_fusion.4
  171.0 0.2 copy.39
  171.3 3.9 %collective-permute-start.3 = (bf16[63,1024]{1,0:T(8,128)(2,1)S(1)}, bf16[63,1024]{1,0:T(8,128)(2,1)S(1)}, u32[]{:S(2)}, u32[]{:S(2)}) collective-permute-start(bf16[63,1024]{1,0:T(8,128)(2,1)S(1)} %slice.72), channel_id=1, source_target_pairs={{0,16},{1,17},{2,18},{3,19},{4,20},{5,21},{6,22},{7,23},{8,24},{9,... | collective-permute-start | bytes 387080 | tf_op jit(solution)/shard_map/ppermute | solution.py:16
  175.3 0.0 collective-permute-done.1
  175.3 1.7 maximum_bitcast_fusion.2
  176.9 6.8 %collective-permute-done.3 = bf16[63,1024]{1,0:T(8,128)(2,1)S(1)} collective-permute-done((bf16[63,1024]{1,0:T(8,128)(2,1)S(1)}, bf16[63,1024]{1,0:T(8,128)(2,1)S(1)}, u32[]{:S(2)}, u32[]{:S(2)}) %collective-permute-start.3) | collective-permute-done | bytes 129056 | tf_op jit(solution)/shard_map/ppermute | solution.py:16
  183.8 0.7 maximum_bitcast_fusion.5
  184.5 0.0 all-to-all-done.5
  184.5 1.0 copy.66
  185.5 2.3 %copy.67 = bf16[1,2,1,16,128,128]{5,4,3,2,1,0:T(8,128)(2,1)} copy(bf16[1,2,1,16,128,128]{5,4,3,2,1,0:T(8,128)(2,1)} %bitcast.37) | data formatting | bytes 2097152
  (42 shorter events, 0.5 us)
Async XLA Ops:
  0.6 44.9 %copy-start = (s32[1,4,2]{1,2,0:T(2,128)S(1)}, s32[1,4,2]{1,2,0:T(2,128)}, u32[]{:S(2)}) copy-start(s32[1,4,2]{1,2,0:T(2,128)} %param.9) | copy-start | bytes 100
  0.6 22.9 %copy-start.11 = (bf16[1,128,1024]{2,1,0:T(8,128)(2,1)S(1)}, bf16[1,128,1024]{2,1,0:T(8,128)(2,1)}, u32[]{:S(2)}) copy-start(bf16[1,128,1024]{2,1,0:T(8,128)(2,1)} %param.8) | copy-start | bytes 786436
  0.7 24.2 %copy-start.10 = (bf16[1,128,1024]{2,1,0:T(8,128)(2,1)S(1)}, bf16[1,128,1024]{2,1,0:T(8,128)(2,1)}, u32[]{:S(2)}) copy-start(bf16[1,128,1024]{2,1,0:T(8,128)(2,1)} %param.5) | copy-start | bytes 786436
  19.1 19.5 %all-to-all-start.2 = ((bf16[1,2,1,16,128,128]{5,4,3,2,0,1:T(8,128)(2,1)}), bf16[1,2,1,16,128,128]{5,4,3,2,0,1:T(8,128)(2,1)}, u32[]{:S(2)}, u32[]{:S(2)}) async-start(bf16[1,2,1,16,128,128]{5,4,3,2,0,1:T(8,128)(2,1)} %bitcast.9), calls=%async_computation.2 | async-start | bytes 2097152 | tf_op jit(solution)/shard_map/all_to_all | solution.py:128
  23.6 22.3 %collective-permute-start.2 = (bf16[1,63,1024]{2,1,0:T(8,128)(2,1)S(1)}, bf16[1,63,1024]{2,1,0:T(8,128)(2,1)S(1)}, u32[]{:S(2)}, u32[]{:S(2)}) collective-permute-start(bf16[1,63,1024]{2,1,0:T(8,128)(2,1)S(1)} %slice.57), channel_id=1, source_target_pairs={{16,0},{17,1},{18,2},{19,3},{20,4},{21,5},{22,6},{23,7},{24,8},{25... | collective-permute-start | bytes 387080 | tf_op jit(solution)/shard_map/ppermute | solution.py:16
  24.9 20.8 %collective-permute-start = (bf16[1,63,1024]{2,1,0:T(8,128)(2,1)S(1)}, bf16[1,63,1024]{2,1,0:T(8,128)(2,1)S(1)}, u32[]{:S(2)}, u32[]{:S(2)}) collective-permute-start(bf16[1,63,1024]{2,1,0:T(8,128)(2,1)S(1)} %slice.49), channel_id=1, source_target_pairs={{16,0},{17,1},{18,2},{19,3},{20,4},{21,5},{22,6},{23,7},{24,8},{25... | collective-permute-start | bytes 387080 | tf_op jit(solution)/shard_map/ppermute | solution.py:16
  38.7 24.8 %all-to-all-start.1 = ((bf16[1,1,1,32,128,128]{5,4,2,1,0,3:T(8,128)(2,1)}), bf16[1,1,1,32,128,128]{5,4,2,1,0,3:T(8,128)(2,1)S(1)}, u32[]{:S(2)}, u32[]{:S(2)}) async-start(bf16[1,1,1,32,128,128]{5,4,2,1,0,3:T(8,128)(2,1)} %bitcast.6), calls=%async_computation.1 | async-start | bytes 2097152 | tf_op jit(solution)/shard_map/all_to_all | solution.py:120
  63.4 27.5 %all-to-all-start.3 = ((bf16[1,1,1,32,128,128]{5,4,2,1,0,3:T(8,128)(2,1)}), bf16[1,1,1,32,128,128]{5,4,2,1,0,3:T(8,128)(2,1)S(1)}, u32[]{:S(2)}, u32[]{:S(2)}) async-start(bf16[1,1,1,32,128,128]{5,4,2,1,0,3:T(8,128)(2,1)} %bitcast.11), calls=%async_computation.3 | async-start | bytes 2097152 | tf_op jit(solution)/shard_map/all_to_all | solution.py:127
  71.0 1.1 copy-start.1
  71.1 1.7 copy-start.7
  71.1 1.7 copy-start.9
  73.0 0.8 copy-start.3
  73.0 17.9 %copy-start.13 = (f32[2,2,8,64]{3,2,1,0:T(8,128)}, f32[2,2,8,64]{3,2,1,0:T(8,128)S(1)}, u32[]{:S(2)}) copy-start(f32[2,2,8,64]{3,2,1,0:T(8,128)S(1)} %sub.66) | copy-start | bytes 24580
  90.9 29.6 %all-to-all-start.6 = ((bf16[1,1,4,8,128,128]{5,4,3,1,0,2:T(8,128)(2,1)}), bf16[1,1,4,8,128,128]{5,4,3,1,0,2:T(8,128)(2,1)}, u32[]{:S(2)}, u32[]{:S(2)}) async-start(bf16[1,1,4,8,128,128]{5,4,3,1,0,2:T(8,128)(2,1)} %fusion.4), calls=%async_computation.6 | async-start | bytes 2097152 | tf_op jit(solution)/shard_map/all_to_all | solution.py:155
  97.5 2.3 %copy-start.4 = (bf16[2,2,8,64,128]{4,3,2,1,0:T(8,128)(2,1)S(1)}, bf16[2,2,8,64,128]{4,3,2,1,0:T(8,128)(2,1)}, u32[]{:S(2)}) copy-start(bf16[2,2,8,64,128]{4,3,2,1,0:T(8,128)(2,1)} %copy-done.3) | copy-start | bytes 1572868
  97.5 2.3 %copy-start.14 = (f32[2,2,8,64]{3,2,1,0:T(8,128)S(1)}, f32[2,2,8,64]{3,2,1,0:T(8,128)}, u32[]{:S(2)}) copy-start(f32[2,2,8,64]{3,2,1,0:T(8,128)} %copy-done.13) | copy-start | bytes 24580
  98.5 3.1 %copy-start.8 = (bf16[2,2,8,64,128]{4,3,2,1,0:T(8,128)(2,1)S(1)}, bf16[2,2,8,64,128]{4,3,2,1,0:T(8,128)(2,1)}, u32[]{:S(2)}) copy-start(bf16[2,2,8,64,128]{4,3,2,1,0:T(8,128)(2,1)} %copy-done.7) | copy-start | bytes 1572868
  100.8 0.8 copy-start.5
  101.6 0.8 copy-start.12
  148.9 10.2 %copy-start.2 = (bf16[4,8,128,64]{3,2,1,0:T(8,128)(2,1)S(1)}, bf16[4,8,128,64]{3,2,1,0:T(8,128)(2,1)}, u32[]{:S(2)}) copy-start(bf16[4,8,128,64]{3,2,1,0:T(8,128)(2,1)} %copy-done.1) | copy-start | bytes 1572868
  148.9 10.2 %copy-start.6 = (bf16[4,8,64,128]{3,2,1,0:T(8,128)(2,1)S(1)}, bf16[4,8,64,128]{3,2,1,0:T(8,128)(2,1)}, u32[]{:S(2)}) copy-start(bf16[4,8,64,128]{3,2,1,0:T(8,128)(2,1)} %copy-done.5) | copy-start | bytes 1572868
  148.9 18.1 %all-to-all-start.7 = ((bf16[1,1,1,32,128,128]{5,4,2,1,0,3:T(8,128)(2,1)}), bf16[1,1,1,32,128,128]{5,4,2,1,0,3:T(8,128)(2,1)}, u32[]{:S(2)}, u32[]{:S(2)}) async-start(bf16[1,1,1,32,128,128]{5,4,2,1,0,3:T(8,128)(2,1)} %bitcast.35), calls=%async_computation.7 | async-start | bytes 2097152 | tf_op jit(solution)/shard_map/all_to_all | solution.py:159
  154.4 16.2 %copy-start.15 = (f32[64,64]{1,0:T(8,128)S(1)}, f32[64,64]{1,0:T(8,128)}, u32[]{:S(2)}) copy-start(f32[64,64]{1,0:T(8,128)} %get-tuple-element.23) | copy-start | bytes 49156
  154.4 20.9 %collective-permute-start.1 = (bf16[63,1024]{1,0:T(8,128)(2,1)}, bf16[63,1024]{1,0:T(8,128)(2,1)}, u32[]{:S(2)}, u32[]{:S(2)}) collective-permute-start(bf16[63,1024]{1,0:T(8,128)(2,1)} %slice.68), channel_id=1, source_target_pairs={{0,16},{1,17},{2,18},{3,19},{4,20},{5,21},{6,22},{7,23},{8,24},{9,... | collective-permute-start | bytes 387080 | tf_op jit(solution)/shard_map/ppermute | solution.py:16
  167.0 17.5 %all-to-all-start.5 = ((bf16[1,1,1,32,128,128]{5,4,2,1,0,3:T(8,128)(2,1)}), bf16[1,1,1,32,128,128]{5,4,2,1,0,3:T(8,128)(2,1)S(1)}, u32[]{:S(2)}, u32[]{:S(2)}) async-start(bf16[1,1,1,32,128,128]{5,4,2,1,0,3:T(8,128)(2,1)} %bitcast.107), calls=%async_computation.5 | async-start | bytes 2097152 | tf_op jit(solution)/shard_map/all_to_all | solution.py:158
  171.3 12.5 %collective-permute-start.3 = (bf16[63,1024]{1,0:T(8,128)(2,1)S(1)}, bf16[63,1024]{1,0:T(8,128)(2,1)S(1)}, u32[]{:S(2)}, u32[]{:S(2)}) collective-permute-start(bf16[63,1024]{1,0:T(8,128)(2,1)S(1)} %slice.72), channel_id=1, source_target_pairs={{0,16},{1,17},{2,18},{3,19},{4,20},{5,21},{6,22},{7,23},{8,24},{9,... | collective-permute-start | bytes 387080 | tf_op jit(solution)/shard_map/ppermute | solution.py:16
where the time goes:
time: 191 us; the launch traced here: 188 us
  waiting for transfers between devices  72.7 us (38%)
  blocking collectives  46.9 us (25%)
  starting transfers between devices  41.3 us (22%)
  other arithmetic  9.99 us (5%)
  local copies, waits for them, and re-layouts  9.59 us (5%)
  matrix products  6.2 us (3%)
    all_to_all x1, blocking collectives, shards(): lax.all_to_all(key_back, 'tp', split_axis=2, concat_axis=3, tiled=True)  28.4 us
    all_to_all x1, blocking collectives, shards(): lax.all_to_all(keys, 'ctx', split_axis=1, concat_axis=3, tiled=True)  18.5 us
    all_to_all x1, waiting for transfers between devices, shards(): lax.all_to_all(value_back, 'tp', split_axis=2, concat_axis=3, tiled=True)  16.6 us
    all_to_all x1, waiting for transfers between devices, shards(): lax.all_to_all(lax.all_to_all(values, 'ctx', split_axis=1, concat_axis=3,...  15 us
    all_to_all x1, waiting for transfers between devices, shards(): lax.all_to_all(lax.all_to_all(keys, 'ctx', split_axis=1, concat_axis=3, t...  14.6 us
    all_to_all x1, waiting for transfers between devices, shards(): lax.all_to_all(values, 'ctx', split_axis=1, concat_axis=3, tiled=True)  12.4 us
    ppermute x4, starting transfers between devices, from_behind(): return lax.ppermute(block, axis, route)  11.2 us
    all_to_all x1, waiting for transfers between devices, shards(): lax.all_to_all(swapped[1], 'ctx', split_axis=3, concat_axis=1, tiled=True)  7.22 us
  transfers between devices with their start and end apart: 10, of which 6 were waited for; matrix products, arithmetic and copies ran while one was open for 11% of the time, Pallas kernels for 0%

commit v1 on v0

v1 whole, which is shorter than its diff:
```python
import functools
import math

import jax
import jax.numpy as jnp
import numpy as np
from jax import lax
from jax.experimental import pallas as pl
from jax.experimental.pallas import tpu as pltpu
from jax.sharding import PartitionSpec as P

DH = 128
SPAN = 64
NBR = 2
TAIL = 16
PAD = TAIL + SPAN
MESH = pl.DeviceIdType.MESH
BF16 = jnp.bfloat16
F32 = jnp.float32


def rotation_tables(rows):
    frequency = 10000.0 ** (-2.0 * np.arange(DH // 2) / DH)
    frequency = frequency.astype(np.float32)
    angles = np.arange(rows, dtype=np.float32)[:, None] * frequency[None, :]
    cosine, sine = np.cos(angles), np.sin(angles)
    return (
        np.concatenate([cosine, cosine], axis=1).astype(np.float32),
        np.concatenate([-sine, sine], axis=1).astype(np.float32),
    )


def dot(a, b, ca, cb):
    return lax.dot_general(a, b, (((ca,), (cb,)), ((), ())), preferred_element_type=F32)


def kernel(
    n_ctx, n_tp, blocks, hc, ht,
    lengths, queries, cotangent, keys, values, cos_ref, sin_ref,
    att_out, gq_out, gk_out, gv_out,
    rin, kbuf, vbuf, gkbuf, gvbuf, qw, gw, ebuf, pbuf, dpbuf, mtile, stat, pstat, sback, bmain, btail,
    in_send, in_recv, st_send, st_recv, bk_send, bk_recv, kv_sem, out_sem,
):
    g = min(hc, ht)
    nbc, nbt = hc // g, ht // g
    units = n_ctx * nbc
    wide = g * DH
    scale = 1.0 / math.sqrt(DH)
    me_c, me_t = lax.axis_index("ctx"), lax.axis_index("tp")
    w, n = me_t // NBR, me_t % NBR
    tokens = (queries, cotangent)
    unroll = 4 if g % 4 == 0 else 1

    def remote(src, dst, send, recv, c, t):
        return pltpu.make_async_remote_copy(
            src_ref=src, dst_ref=dst, send_sem=send, recv_sem=recv,
            device_id={"ctx": c, "tp": t}, device_id_type=MESH,
        )

    def arrive(dst, recv):
        pltpu.make_async_copy(dst, dst, recv).wait()

    def is_me(c, t):
        return jnp.logical_and(c == me_c, t == me_t)

    def kv_copies(c):
        return (
            pltpu.make_async_copy(keys.at[c], kbuf.at[c], kv_sem.at[0, c]),
            pltpu.make_async_copy(values.at[c], vbuf.at[c], kv_sem.at[1, c]),
        )

    @pl.loop(0, n_ctx)
    def _(c):
        for copy in kv_copies(c):
            copy.start()

    barrier = pltpu.get_barrier_semaphore()

    @pl.loop(0, n_ctx * n_tp)
    def _(i):
        c, t = i // n_tp, i % n_tp

        @pl.when(jnp.logical_not(is_me(c, t)))
        def _():
            pl.semaphore_signal(barrier, inc=1, device_id={"ctx": c, "tp": t}, device_id_type=MESH)

    pl.semaphore_wait(barrier, n_ctx * n_tp - 1)

    def in_sends(act):
        for t in reversed(range(n_tp)):
            tw = t // NBR
            for kb in range(nbt):
                first = me_t * ht + kb * g
                c = first // hc
                sb = (first % hc) // g
                for a in range(2):
                    for piece in range(2):
                        ok = True
                        if piece == 0:
                            rows, slot, spot = pl.ds((tw + 1) * SPAN - TAIL, TAIL), me_c, pl.ds(0, TAIL)
                        elif tw < blocks - 1:
                            rows, slot, spot = pl.ds((tw + 1) * SPAN, SPAN), me_c, pl.ds(TAIL, SPAN)
                        else:
                            rows, slot, spot = pl.ds(0, SPAN), me_c - 1, pl.ds(TAIL, SPAN)
                            ok = me_c > 0
                        slot = jnp.maximum(slot, 0)
                        src = tokens[a].at[rows, pl.ds(kb * wide, wide)]
                        unit = slot * nbc + sb
                        dst = rin.at[a, unit, spot]
                        send, recv = in_send.at[a, t, kb, piece], in_recv.at[a, unit, piece]
                        act(src, dst, send, recv, c, t, ok)

    def start(src, dst, send, recv, c, t, ok):
        mine = is_me(c, t)

        @pl.when(jnp.logical_and(ok, mine))
        def _():
            pltpu.make_async_copy(src, dst, recv).start()

        @pl.when(jnp.logical_and(ok, jnp.logical_not(mine)))
        def _():
            remote(src, dst, send, recv, c, t).start()

    def sent(src, dst, send, recv, c, t, ok):
        @pl.when(jnp.logical_and(ok, jnp.logical_not(is_me(c, t))))
        def _():
            remote(src, dst, send, recv, c, t).wait_send()

    in_sends(start)

    def rotated(x, rows, sign):
        turned = pltpu.roll(x, DH // 2, 1) * sin_ref[:rows]
        return x * cos_ref[:rows] + (turned if sign > 0 else -turned)

    def order(k):
        return (me_c + k) % n_ctx

    @pl.loop(0, n_ctx)
    def _(k):
        c = order(k)
        for copy in kv_copies(c):
            copy.wait()

        @pl.loop(0, hc // unroll)
        def _(hg):
            for i in range(unroll):
                h = hg * unroll + i
                x = kbuf[c, h].astype(F32)
                kbuf[c, h] = rotated(x, x.shape[0], 1).astype(BF16)

    lane = lax.broadcasted_iota(jnp.int32, (SPAN, DH), 1)
    half = DH // 2

    def partner_sends(unit, act):
        for i in range(1, NBR):
            t = w * NBR + (n + i) % NBR
            copy = remote(
                stat.at[unit], pstat.at[unit, i - 1], st_send.at[unit, i - 1], st_recv.at[unit, i - 1], me_c, t
            )
            act(copy)

    @pl.loop(0, units)
    def _(k):
        c = order(k // nbc)
        sb = k % nbc
        unit = c * nbc + sb
        missing = jnp.logical_and(w == blocks - 1, c == n_ctx - 1)
        for a in range(2):
            arrive(rin.at[a, unit, pl.ds(0, TAIL)], in_recv.at[a, unit, 0])

            @pl.when(jnp.logical_not(missing))
            def _():
                arrive(rin.at[a, unit, pl.ds(TAIL, SPAN)], in_recv.at[a, unit, 1])

            @pl.when(missing)
            def _():
                rin[a, unit, TAIL:PAD] = jnp.zeros((SPAN, wide), BF16)

        count = lengths[c * blocks + w, n]
        live = lane[:, :] < count
        stat[unit] = jnp.zeros((SPAN, DH), F32)
        mtile[unit] = jnp.zeros((SPAN, DH), F32)

        @pl.loop(0, g // unroll)
        def _(hg):
            lps, ds, ms = [], [], []
            for i in range(unroll):
                hh = hg * unroll + i
                h = sb * g + hh
                at = c * hc + h
                columns = pl.ds(pl.multiple_of(hh * DH, DH), DH)

                def window(a):
                    raw = rin[a, unit, :, columns].astype(F32)
                    return pltpu.roll(raw, PAD - (TAIL - 1), 0)[:SPAN]

                q = rotated(window(0), SPAN, 1).astype(BF16)
                grad32 = window(1)
                grad = grad32.astype(BF16)
                qw[at] = q
                gw[at] = grad
                s = dot(q, kbuf[c, h], 1, 1) * scale
                s = jnp.where(live, s, -jnp.inf)
                m = jnp.max(s, axis=1, keepdims=True)
                e = jnp.exp(s - m)
                total = jnp.sum(e, axis=1, keepdims=True)
                value = vbuf[c, h]
                part = dot(e.astype(BF16), value, 1, 0)
                ebuf[at] = e
                pbuf[at] = part
                dpbuf[at] = dot(grad, value, 1, 1)
                lps.append(m + jnp.log(total))
                ds.append(jnp.sum(grad32 * part, axis=1, keepdims=True) / total)
                ms.append(m)
            st, mt = stat[unit], mtile[unit]
            for i in range(unroll):
                hh = hg * unroll + i
                st = jnp.where(lane == hh, lps[i], st)
                st = jnp.where(lane == hh + half, ds[i], st)
                mt = jnp.where(lane == hh, ms[i], mt)
            stat[unit] = st
            mtile[unit] = mt

        partner_sends(unit, lambda copy: copy.start())

    def back_sends(c, sb, act):
        unit = c * nbc + sb
        first = me_c * hc + sb * g
        t = first // ht
        kb = (first % ht) // g
        columns = pl.ds(pl.multiple_of(kb * wide, DH), wide)
        for a in range(2):
            for piece in range(2):
                if piece == 0:
                    src, dst = sback.at[a, unit, pl.ds(0, TAIL)], btail.at[a, n, w, :, columns]
                    to, ok, recv = c, True, bk_recv.at[a, n, w, kb, 0]
                else:
                    j = jnp.where(w == blocks - 1, 0, w + 1)
                    src, dst = sback.at[a, unit, pl.ds(TAIL, SPAN)], bmain.at[a, n, j, :, columns]
                    to = jnp.where(w == blocks - 1, c + 1, c)
                    ok = to < n_ctx
                    to = jnp.minimum(to, n_ctx - 1)
                    recv = bk_recv.at[a, n, j, kb, 1]
                act(src, dst, bk_send.at[a, unit, piece], recv, to, t, ok)

    def out_copies(c, sb):
        heads = pl.ds(sb * g, g)
        return (
            pltpu.make_async_copy(gkbuf.at[c, heads], gk_out.at[c, heads], out_sem.at[0, c, sb]),
            pltpu.make_async_copy(gvbuf.at[c, heads], gv_out.at[c, heads], out_sem.at[1, c, sb]),
        )

    @pl.loop(0, units)
    def _(k):
        c = order(k // nbc)
        sb = k % nbc
        unit = c * nbc + sb
        partner_sends(unit, lambda copy: copy.wait_recv())
        own = stat[unit]
        others = [pstat[unit, i] for i in range(NBR - 1)]
        top = functools.reduce(jnp.maximum, others, own)
        lse = top + jnp.log(sum(jnp.exp(x - top) for x in [own] + others))
        dots = sum(jnp.exp(x - lse) * pltpu.roll(x, half, 1) for x in [own] + others)
        factor = jnp.exp(mtile[unit] - lse)
        both = jnp.where(lane < half, factor, pltpu.roll(dots, half, 1))

        @pl.loop(0, g // unroll)
        def _(hg):
            for i in range(unroll):
                hh = hg * unroll + i
                h = sb * g + hh
                at = c * hc + h
                columns = pl.ds(pl.multiple_of(hh * DH, DH), DH)
                fac = jnp.sum(jnp.where(lane == hh, both, 0.0), axis=1, keepdims=True)
                dcol = jnp.sum(jnp.where(lane == hh + half, both, 0.0), axis=1, keepdims=True)
                pr = ebuf[at] * fac
                gvbuf[c, h] = dot(pr.astype(BF16), gw[at], 0, 0).astype(BF16)
                gs = (pr * (dpbuf[at] - dcol) * scale).astype(BF16)
                gq = dot(gs, kbuf[c, h], 1, 0)
                gk = dot(gs, qw[at], 0, 0)
                gkbuf[c, h] = rotated(gk, gk.shape[0], -1).astype(BF16)
                att = pbuf[at] * fac
                for a, x in ((0, att), (1, gq)):
                    padded = jnp.concatenate([x, jnp.zeros((TAIL, DH), F32)], axis=0)
                    sback[a, unit, :, columns] = pltpu.roll(padded, TAIL - 1, 0).astype(BF16)

        back_sends(c, sb, start)
        for copy in out_copies(c, sb):
            copy.start()

    shifted_cos = pltpu.roll(cos_ref[:SPAN], SPAN - 1, 0)
    shifted_sin = pltpu.roll(sin_ref[:SPAN], SPAN - 1, 0)
    for j in range(blocks):
        for a in range(2):
            for nn in range(NBR):
                for kb in range(nbt):
                    columns = pl.ds(kb * wide, wide)
                    arrive(btail.at[a, nn, j, :, columns], bk_recv.at[a, nn, j, kb, 0])
                    main = bmain.at[a, nn, j, :, columns]
                    recv = bk_recv.at[a, nn, j, kb, 1]
                    if j > 0:
                        arrive(main, recv)
                    else:
                        @pl.when(me_c > 0)
                        def _():
                            arrive(main, recv)

                        @pl.when(me_c == 0)
                        def _():
                            bmain[a, nn, j, :, kb * wide : (kb + 1) * wide] = jnp.zeros((SPAN, wide), BF16)

        @pl.loop(0, ht)
        def _(h):
            columns = pl.ds(pl.multiple_of(h * DH, DH), DH)

            def gathered(a):
                main = sum(bmain[a, nn, j, :, columns].astype(F32) for nn in range(NBR))
                tail = sum(btail[a, nn, j, :, columns].astype(F32) for nn in range(NBR))
                return jnp.concatenate([main[: SPAN - TAIL], main[SPAN - TAIL :] + tail], axis=0)

            rows = pl.ds(j * SPAN, SPAN)
            att_out[rows, columns] = gathered(0).astype(BF16)
            x = gathered(1)
            x = x * shifted_cos - pltpu.roll(x, DH // 2, 1) * shifted_sin
            gq_out[rows, columns] = x.astype(BF16)

    in_sends(sent)

    @pl.loop(0, units)
    def _(k):
        c, sb = k // nbc, k % nbc
        partner_sends(c * nbc + sb, lambda copy: copy.wait_send())
        back_sends(c, sb, sent)
        for copy in out_copies(c, sb):
            copy.wait()


def shards(n_ctx, n_tp, queries, keys, values, cotangent, lengths):
    rows, width = queries.shape[1:]
    blocks = rows // SPAN
    ht = width // DH
    hc, neigh = keys.shape[3], keys.shape[4]
    assert keys.shape[2] == 1 and blocks * NBR == n_tp
    g = min(hc, ht)
    nbc, nbt = hc // g, ht // g
    units, wide = n_ctx * nbc, g * DH
    cosine, sine = rotation_tables(max(neigh, SPAN))
    kv_shape = (n_ctx, hc, neigh, DH)
    heads = n_ctx * hc
    any_space = pl.BlockSpec(memory_space=pl.ANY)
    vmem = pl.BlockSpec(memory_space=pltpu.VMEM)
    dma = pltpu.SemaphoreType.DMA
    att, gq, gk, gv = pl.pallas_call(
        functools.partial(kernel, n_ctx, n_tp, blocks, hc, ht),
        out_shape=(
            jax.ShapeDtypeStruct((rows, width), BF16),
            jax.ShapeDtypeStruct((rows, width), BF16),
            jax.ShapeDtypeStruct(kv_shape, BF16),
            jax.ShapeDtypeStruct(kv_shape, BF16),
        ),
        in_specs=[pl.BlockSpec(memory_space=pltpu.SMEM), vmem, vmem, any_space, any_space, vmem, vmem],
        out_specs=(vmem, vmem, any_space, any_space),
        scratch_shapes=[
            pltpu.VMEM((2, units, PAD, wide), BF16),
            pltpu.VMEM(kv_shape, BF16),
            pltpu.VMEM(kv_shape, BF16),
            pltpu.VMEM(kv_shape, BF16),
            pltpu.VMEM(kv_shape, BF16),
            pltpu.VMEM((heads, SPAN, DH), BF16),
            pltpu.VMEM((heads, SPAN, DH), BF16),
            pltpu.VMEM((heads, SPAN, neigh), F32),
            pltpu.VMEM((heads, SPAN, DH), F32),
            pltpu.VMEM((heads, SPAN, neigh), F32),
            pltpu.VMEM((units, SPAN, DH), F32),
            pltpu.VMEM((units, SPAN, DH), F32),
            pltpu.VMEM((units, NBR - 1, SPAN, DH), F32),
            pltpu.VMEM((2, units, PAD, wide), BF16),
            pltpu.VMEM((2, NBR, blocks, SPAN, width), BF16),
            pltpu.VMEM((2, NBR, blocks, TAIL, width), BF16),
            dma((2, n_tp, nbt, 2)),
            dma((2, units, 2)),
            dma((units, NBR - 1)),
            dma((units, NBR - 1)),
            dma((2, units, 2)),
            dma((2, NBR, blocks, nbt, 2)),
            dma((2, n_ctx)),
            dma((2, n_ctx, nbc)),
        ],
        compiler_params=pltpu.CompilerParams(
            collective_id=0, has_side_effects=True, vmem_limit_bytes=48 * 1024 * 1024
        ),
    )(
        lengths[0].reshape(-1, NBR),
        queries[0],
        cotangent[0],
        keys.reshape(kv_shape),
        values.reshape(kv_shape),
        jnp.asarray(cosine),
        jnp.asarray(sine),
    )
    return (att[None], gq[None], gk.reshape(keys.shape), gv.reshape(values.shape))


def solution(mesh):
    tok = P("dp", "ctx", "tp")
    kv = P("dp", None, "tp", "ctx", None, None)
    return jax.shard_map(
        functools.partial(shards, mesh.shape["ctx"], mesh.shape["tp"]),
        mesh=mesh,
        in_specs=(tok, kv, kv, tok, P("dp", None, None)),
        out_specs=(tok, tok, kv, kv),
        check_vma=False,
    )
```

time: 191 us -> 109 us (0.57); the launches traced: 188 us -> 108 us
  Pallas kernels: 0 us -> 97.4 us
  waiting for transfers between devices: 72.7 us -> 0 us
  blocking collectives: 46.9 us -> 0 us
  starting transfers between devices: 41.3 us -> 0 us
  other arithmetic: 9.99 us -> 0 us
  matrix products: 6.2 us -> 0 us
    pallas_call x0 -> x1, Pallas kernels: none -> 97.4 us  [shards(): pl.pallas_call(functools.partial(kernel, n_ctx, n_tp, blocks, hc, ht), ou...]
    all_to_all x6 -> x0, waiting for transfers between devices: 65.9 us -> none  [the longest x1 16.6 us: shards(): lax.all_to_all(value_back, 'tp', split_axis=2, concat_axis=3, tiled=True)]
    all_to_all x2 -> x0, blocking collectives: 46.9 us -> none  [the longest x1 28.4 us: shards(): lax.all_to_all(key_back, 'tp', split_axis=2, concat_axis=3, tiled=True)]
    all_to_all x6 -> x0, starting transfers between devices: 30.1 us -> none  [the longest x1 6.58 us: shards(): lax.all_to_all(value_back, 'tp', split_axis=2, concat_axis=3, tiled=True)]
    ppermute x4 -> x0, starting transfers between devices: 11.2 us -> none  [from_behind(): return lax.ppermute(block, axis, route)]
    ppermute x4 -> x0, waiting for transfers between devices: 6.85 us -> none  [from_behind(): return lax.ppermute(block, axis, route)]
    dot_general x6 -> x0, matrix products: 6.2 us -> none  [the longest x1 2.02 us: neighbour_backward(): jnp.einsum('zhij,zhid->zhjd', chances.astype(jnp.bfloat16), grad_rows, pr...]
    unnamed x38 -> x18, local copies, waits for them, and re-layouts: 6.15 us -> 10 us
  transfers between devices with their start and end apart: 10 -> 0, of which waited for: 6 -> 0; matrix products, arithmetic and copies ran while one was open for 11% -> 0% of each run, Pallas kernels for 0% -> 0%
where the time goes in v1:
time: 109 us; the launch traced here: 108 us
  Pallas kernels  97.4 us (89%)
  local copies, waits for them, and re-layouts  10.1 us (9%)
    pallas_call x1, Pallas kernels, shards(): pl.pallas_call(functools.partial(kernel, n_ctx, n_tp, blocks, hc, ht), ou...  97.4 us
    unnamed x18, local copies, waits for them, and re-layouts  10 us

profile of v1, /device:TPU:24, one launch (start us, length us, event | category | flops | bytes accessed | tf_op | source)
XLA Modules:
  0.0 108.1 jit_solution(9926213230646209945)
XLA Ops:
  0.6 0.0 copy-start.6
  0.6 0.7 copy-done.6
  1.3 0.1 copy.11.lengths
  1.4 0.0 copy-start
  1.4 1.2 %copy-done = bf16[1,2,1,16,128,128]{5,4,3,2,1,0:T(8,128)(2,1)S(1)} copy-done((bf16[1,2,1,16,128,128]{5,4,3,2,1,0:T(8,128)(2,1)S(1)}, bf16[1,2,1,16,128,128]{5,4,3,2,1,0:T(8,128)(2,1)}, u32[]{:S(2)}) %copy-start) | copy-done | bytes 1048600
  2.6 0.0 copy-start.1
  2.6 1.2 %copy-done.1 = bf16[1,2,1,16,128,128]{5,4,3,2,1,0:T(8,128)(2,1)S(1)} copy-done((bf16[1,2,1,16,128,128]{5,4,3,2,1,0:T(8,128)(2,1)S(1)}, bf16[1,2,1,16,128,128]{5,4,3,2,1,0:T(8,128)(2,1)}, u32[]{:S(2)}) %copy-start.1) | copy-done | bytes 1048600
  3.9 0.0 copy-start.2
  3.9 0.9 copy-done.2
  4.8 0.0 copy-start.3
  4.8 0.9 copy-done.3
  5.8 0.0 copy-start.4
  5.8 0.8 copy-done.4
  6.6 0.0 copy-start.5
  6.6 0.8 copy-done.5
  7.4 97.4 %shard_map.102 = (bf16[128,1024]{1,0:T(8,128)(2,1)S(1)}, bf16[128,1024]{1,0:T(8,128)(2,1)S(1)}, bf16[2,16,128,128]{3,2,1,0:T(8,128)(2,1)S(1)}, bf16[2,16,128,128]{3,2,1,0:T(8,128)(2,1)S(1)}) custom-call(s32[4,2]{1,0:T(4,128)S(1)} %copy.11.lengths, bf16[128,1024]{1,0:T(8,128)(2,1)S(1)} %bitcast.17, bf16[128,1024]{1,0:T(8,128)(2,1)S(1)} %bitcast.18, ...), custom_call_target="tpu_custom_call" | custom-call | tf_op jit(solution)/shard_map/pallas_call | solution.py:353
  104.8 0.7 copy.18
  105.5 0.7 copy.19
  106.2 1.0 copy.20
  107.2 1.0 copy.21
Async XLA Ops:
  0.6 0.7 copy-start.6
  1.4 1.2 %copy-start = (bf16[1,2,1,16,128,128]{5,4,3,2,1,0:T(8,128)(2,1)S(1)}, bf16[1,2,1,16,128,128]{5,4,3,2,1,0:T(8,128)(2,1)}, u32[]{:S(2)}) copy-start(bf16[1,2,1,16,128,128]{5,4,3,2,1,0:T(8,128)(2,1)} %param.8) | copy-start | bytes 3145732
  2.6 1.2 %copy-start.1 = (bf16[1,2,1,16,128,128]{5,4,3,2,1,0:T(8,128)(2,1)S(1)}, bf16[1,2,1,16,128,128]{5,4,3,2,1,0:T(8,128)(2,1)}, u32[]{:S(2)}) copy-start(bf16[1,2,1,16,128,128]{5,4,3,2,1,0:T(8,128)(2,1)} %param.9) | copy-start | bytes 3145732
  3.9 0.9 copy-start.2
  4.8 0.9 copy-start.3
  5.8 0.8 copy-start.4
  6.6 0.8 copy-start.5

commit v2 on v1

--- a/solution.py
+++ b/solution.py
@@ -12,8 +12,6 @@
 DH = 128
 SPAN = 64
 NBR = 2
-TAIL = 16
-PAD = TAIL + SPAN
 MESH = pl.DeviceIdType.MESH
 BF16 = jnp.bfloat16
 F32 = jnp.float32
@@ -36,10 +34,12 @@
 
 def kernel(
     n_ctx, n_tp, blocks, hc, ht,
-    lengths, queries, cotangent, keys, values, cos_ref, sin_ref,
+    lengths, queries, cotangent, keys, values, tables_in,
     att_out, gq_out, gk_out, gv_out,
-    rin, kbuf, vbuf, gkbuf, gvbuf, qw, gw, ebuf, pbuf, dpbuf, mtile, stat, pstat, sback, bmain, btail,
-    in_send, in_recv, st_send, st_recv, bk_send, bk_recv, kv_sem, out_sem,
+    tokens, tables, firsts, stage, rfirst, ffirst, rin, kbuf, vbuf, gkbuf, gvbuf, qw, gw, ebuf, pbuf, dpbuf,
+    mtile, stat, pstat, sback, fback, tback, bmain, btail,
+    z_send, z_recv, relay_send, x_send, x_recv, f_send, f_recv, st_send, st_recv, bk_send, bk_recv,
+    tok_sem, kv_sem, out_sem,
 ):
     g = min(hc, ht)
     nbc, nbt = hc // g, ht // g
@@ -48,7 +48,7 @@
     scale = 1.0 / math.sqrt(DH)
     me_c, me_t = lax.axis_index("ctx"), lax.axis_index("tp")
     w, n = me_t // NBR, me_t % NBR
-    tokens = (queries, cotangent)
+    cos_ref, sin_ref = tables.at[0], tables.at[1]
     unroll = 4 if g % 4 == 0 else 1
 
     def remote(src, dst, send, recv, c, t):
@@ -69,6 +69,14 @@
             pltpu.make_async_copy(values.at[c], vbuf.at[c], kv_sem.at[1, c]),
         )
 
+    first_copies = (
+        pltpu.make_async_copy(queries, tokens.at[0], tok_sem.at[0]),
+        pltpu.make_async_copy(cotangent, tokens.at[1], tok_sem.at[1]),
+        pltpu.make_async_copy(tables_in, tables, tok_sem.at[2]),
+    )
+    for copy in first_copies:
+        copy.start()
+
     @pl.loop(0, n_ctx)
     def _(c):
         for copy in kv_copies(c):
@@ -84,31 +92,17 @@
         def _():
             pl.semaphore_signal(barrier, inc=1, device_id={"ctx": c, "tp": t}, device_id_type=MESH)
 
+    for copy in first_copies:
+        copy.wait()
+
+    for a in range(2):
+        for j in range(blocks):
+            row = tokens[a, (j + 1) * SPAN - 16 : (j + 1) * SPAN, :].astype(F32)[15:16]
+            for kb in range(nbt):
+                pieces = [row[:, (kb * g + i) * DH : (kb * g + i + 1) * DH] for i in range(g)]
+                firsts[j, kb, a] = jnp.concatenate(pieces, axis=0).astype(BF16)
+
     pl.semaphore_wait(barrier, n_ctx * n_tp - 1)
-
-    def in_sends(act):
-        for t in reversed(range(n_tp)):
-            tw = t // NBR
-            for kb in range(nbt):
-                first = me_t * ht + kb * g
-                c = first // hc
-                sb = (first % hc) // g
-                for a in range(2):
-                    for piece in range(2):
-                        ok = True
-                        if piece == 0:
-                            rows, slot, spot = pl.ds((tw + 1) * SPAN - TAIL, TAIL), me_c, pl.ds(0, TAIL)
-                        elif tw < blocks - 1:
-                            rows, slot, spot = pl.ds((tw + 1) * SPAN, SPAN), me_c, pl.ds(TAIL, SPAN)
-                        else:
-                            rows, slot, spot = pl.ds(0, SPAN), me_c - 1, pl.ds(TAIL, SPAN)
-                            ok = me_c > 0
-                        slot = jnp.maximum(slot, 0)
-                        src = tokens[a].at[rows, pl.ds(kb * wide, wide)]
-                        unit = slot * nbc + sb
-                        dst = rin.at[a, unit, spot]
-                        send, recv = in_send.at[a, t, kb, piece], in_recv.at[a, unit, piece]
-                        act(src, dst, send, recv, c, t, ok)
 
     def start(src, dst, send, recv, c, t, ok):
         mine = is_me(c, t)
@@ -126,7 +120,81 @@
         def _():
             remote(src, dst, send, recv, c, t).wait_send()
 
-    in_sends(start)
+    def head_block(tq, kb):
+        first = tq * ht + kb * g
+        return first // hc, (first % hc) // g
+
+    def used(tw):
+        return jnp.logical_not(jnp.logical_and(me_c == 0, tw == blocks - 1))
+
+    def near(visit):
+        for d in range(n_tp):
+            for sign in (1, -1) if d else (1,):
+                t = me_t + sign * d
+                visit(jnp.clip(t, 0, n_tp - 1), jnp.logical_and(t >= 0, t < n_tp), d)
+
+    def z_sends(act):
+        def visit(t, ok, d):
+            tw = t // NBR
+            ok = jnp.logical_and(ok, used(tw))
+            block = (tw + 1) % blocks
+            rows = pl.ds(pl.multiple_of(block * SPAN, SPAN), SPAN)
+            for a in range(2):
+                taken = jnp.logical_or(tw == w, t % NBR == a)
+                act(
+                    tokens.at[a, rows], stage.at[a, me_t], z_send.at[a, t], z_recv.at[a, me_t],
+                    me_c, t, jnp.logical_and(ok, taken),
+                )
+
+        near(visit)
+
+    def f_sends(act):
+        for t in range(n_tp):
+            for kb in range(nbt):
+                c, sb = head_block(me_t, kb)
+                act(
+                    firsts.at[t // NBR, kb], rfirst.at[me_c * nbc + sb], f_send.at[t, kb],
+                    f_recv.at[me_c * nbc + sb], c, t, True,
+                )
+
+    slot = jnp.maximum(jnp.where(w == blocks - 1, me_c - 1, me_c), 0)
+    partner = w * NBR + (NBR - 1 - n)
+
+    def x_sends(tq, a, act, ok):
+        for kb in range(nbt):
+            c, sb = head_block(tq, kb)
+            unit = slot * nbc + sb
+            act(
+                stage.at[a, tq, :, pl.ds(kb * wide, wide)], rin.at[a, unit],
+                x_send.at[a, tq, kb], x_recv.at[a, unit], c, me_t, ok,
+            )
+
+    def relay(tq, a):
+        return remote(stage.at[a, tq], stage.at[a, tq], relay_send.at[a, tq], z_recv.at[a, tq], me_c, partner)
+
+    def handle(direct):
+        def visit(tq, ok, d):
+            ok = jnp.logical_and(ok, used(w))
+            inside = tq // NBR == w
+            for a in range(2):
+                straight = jnp.logical_or(inside, n == a)
+                now = jnp.logical_and(ok, straight if direct else jnp.logical_not(straight))
+
+                @pl.when(now)
+                def _():
+                    arrive(stage.at[a, tq], z_recv.at[a, tq])
+
+                if direct:
+                    @pl.when(jnp.logical_and(now, jnp.logical_not(inside)))
+                    def _():
+                        relay(tq, a).start()
+
+                x_sends(tq, a, start, now)
+
+        near(visit)
+
+    z_sends(start)
+    f_sends(start)
 
     def rotated(x, rows, sign):
         turned = pltpu.roll(x, DH // 2, 1) * sin_ref[:rows]
@@ -148,7 +216,11 @@
                 x = kbuf[c, h].astype(F32)
                 kbuf[c, h] = rotated(x, x.shape[0], 1).astype(BF16)
 
+    handle(True)
+    handle(False)
+
     lane = lax.broadcasted_iota(jnp.int32, (SPAN, DH), 1)
+    row_of = lax.broadcasted_iota(jnp.int32, (SPAN, DH), 0)
     half = DH // 2
 
     def partner_sends(unit, act):
@@ -165,16 +237,17 @@
         sb = k % nbc
         unit = c * nbc + sb
         missing = jnp.logical_and(w == blocks - 1, c == n_ctx - 1)
+        arrive(rfirst.at[unit], f_recv.at[unit])
         for a in range(2):
-            arrive(rin.at[a, unit, pl.ds(0, TAIL)], in_recv.at[a, unit, 0])
+            ffirst[a] = rfirst[unit, a].astype(F32)
 
             @pl.when(jnp.logical_not(missing))
             def _():
-                arrive(rin.at[a, unit, pl.ds(TAIL, SPAN)], in_recv.at[a, unit, 1])
+                arrive(rin.at[a, unit], x_recv.at[a, unit])
 
             @pl.when(missing)
             def _():
-                rin[a, unit, TAIL:PAD] = jnp.zeros((SPAN, wide), BF16)
+                rin[a, unit] = jnp.zeros((SPAN, wide), BF16)
 
         count = lengths[c * blocks + w, n]
         live = lane[:, :] < count
@@ -191,8 +264,8 @@
                 columns = pl.ds(pl.multiple_of(hh * DH, DH), DH)
 
                 def window(a):
-                    raw = rin[a, unit, :, columns].astype(F32)
-                    return pltpu.roll(raw, PAD - (TAIL - 1), 0)[:SPAN]
+                    raw = pltpu.roll(rin[a, unit, :, columns].astype(F32), 1, 0)
+                    return jnp.where(row_of == 0, ffirst[a, pl.ds(hh, 1)], raw)
 
                 q = rotated(window(0), SPAN, 1).astype(BF16)
                 grad32 = window(1)
@@ -229,19 +302,16 @@
         t = first // ht
         kb = (first % ht) // g
         columns = pl.ds(pl.multiple_of(kb * wide, DH), wide)
+        j = jnp.where(w == blocks - 1, 0, w + 1)
+        to = jnp.where(w == blocks - 1, c + 1, c)
         for a in range(2):
-            for piece in range(2):
-                if piece == 0:
-                    src, dst = sback.at[a, unit, pl.ds(0, TAIL)], btail.at[a, n, w, :, columns]
-                    to, ok, recv = c, True, bk_recv.at[a, n, w, kb, 0]
-                else:
-                    j = jnp.where(w == blocks - 1, 0, w + 1)
-                    src, dst = sback.at[a, unit, pl.ds(TAIL, SPAN)], bmain.at[a, n, j, :, columns]
-                    to = jnp.where(w == blocks - 1, c + 1, c)
-                    ok = to < n_ctx
-                    to = jnp.minimum(to, n_ctx - 1)
-                    recv = bk_recv.at[a, n, j, kb, 1]
-                act(src, dst, bk_send.at[a, unit, piece], recv, to, t, ok)
+            act(
+                sback.at[a, unit], bmain.at[a, n, j, :, columns], bk_send.at[a, unit, 0],
+                bk_recv.at[a, n, j, kb, 0], jnp.minimum(to, n_ctx - 1), t, to < n_ctx,
+            )
+        act(
+            tback.at[unit], btail.at[n, w, kb], bk_send.at[0, unit, 1], bk_recv.at[0, n, w, kb, 1], c, t, True
+        )
 
     def out_copies(c, sb):
         heads = pl.ds(sb * g, g)
@@ -281,9 +351,12 @@
                 gkbuf[c, h] = rotated(gk, gk.shape[0], -1).astype(BF16)
                 att = pbuf[at] * fac
                 for a, x in ((0, att), (1, gq)):
-                    padded = jnp.concatenate([x, jnp.zeros((TAIL, DH), F32)], axis=0)
-                    sback[a, unit, :, columns] = pltpu.roll(padded, TAIL - 1, 0).astype(BF16)
-
+                    fback[a, pl.ds(hh, 1)] = x[:1]
+                    moved = jnp.where(row_of == SPAN - 1, 0.0, pltpu.roll(x, SPAN - 1, 0))
+                    sback[a, unit, :, columns] = moved.astype(BF16)
+
+        for a in range(2):
+            tback[unit, a] = fback[a].astype(BF16)
         back_sends(c, sb, start)
         for copy in out_copies(c, sb):
             copy.start()
@@ -291,13 +364,12 @@
     shifted_cos = pltpu.roll(cos_ref[:SPAN], SPAN - 1, 0)
     shifted_sin = pltpu.roll(sin_ref[:SPAN], SPAN - 1, 0)
     for j in range(blocks):
-        for a in range(2):
-            for nn in range(NBR):
-                for kb in range(nbt):
-                    columns = pl.ds(kb * wide, wide)
-                    arrive(btail.at[a, nn, j, :, columns], bk_recv.at[a, nn, j, kb, 0])
-                    main = bmain.at[a, nn, j, :, columns]
-                    recv = bk_recv.at[a, nn, j, kb, 1]
+        for nn in range(NBR):
+            for kb in range(nbt):
+                arrive(btail.at[nn, j, kb], bk_recv.at[0, nn, j, kb, 1])
+                for a in range(2):
+                    main = bmain.at[a, nn, j, :, pl.ds(kb * wide, wide)]
+                    recv = bk_recv.at[a, nn, j, kb, 0]
                     if j > 0:
                         arrive(main, recv)
                     else:
@@ -309,22 +381,29 @@
                         def _():
                             bmain[a, nn, j, :, kb * wide : (kb + 1) * wide] = jnp.zeros((SPAN, wide), BF16)
 
-        @pl.loop(0, ht)
-        def _(h):
-            columns = pl.ds(pl.multiple_of(h * DH, DH), DH)
+        for h in range(ht):
+            columns = slice(h * DH, (h + 1) * DH)
 
             def gathered(a):
                 main = sum(bmain[a, nn, j, :, columns].astype(F32) for nn in range(NBR))
-                tail = sum(btail[a, nn, j, :, columns].astype(F32) for nn in range(NBR))
-                return jnp.concatenate([main[: SPAN - TAIL], main[SPAN - TAIL :] + tail], axis=0)
-
-            rows = pl.ds(j * SPAN, SPAN)
+                last = sum(btail[nn, j, h // g, a].astype(F32) for nn in range(NBR))[h % g : h % g + 1]
+                return jnp.where(row_of == SPAN - 1, last, main)
+
+            rows = slice(j * SPAN, (j + 1) * SPAN)
             att_out[rows, columns] = gathered(0).astype(BF16)
             x = gathered(1)
             x = x * shifted_cos - pltpu.roll(x, DH // 2, 1) * shifted_sin
             gq_out[rows, columns] = x.astype(BF16)
 
-    in_sends(sent)
+    z_sends(sent)
+    f_sends(sent)
+    for tq in range(n_tp):
+        for a in range(2):
+            x_sends(tq, a, sent, used(w))
+
+            @pl.when(jnp.logical_and(used(w), jnp.logical_and(tq // NBR != w, n == a)))
+            def _():
+                relay(tq, a).wait_send()
 
     @pl.loop(0, units)
     def _(k):
@@ -358,10 +437,16 @@
             jax.ShapeDtypeStruct(kv_shape, BF16),
             jax.ShapeDtypeStruct(kv_shape, BF16),
         ),
-        in_specs=[pl.BlockSpec(memory_space=pltpu.SMEM), vmem, vmem, any_space, any_space, vmem, vmem],
+        in_specs=[pl.BlockSpec(memory_space=pltpu.SMEM)] + [pl.BlockSpec(memory_space=pltpu.HBM)] * 5,
         out_specs=(vmem, vmem, any_space, any_space),
         scratch_shapes=[
-            pltpu.VMEM((2, units, PAD, wide), BF16),
+            pltpu.VMEM((2, rows, width), BF16),
+            pltpu.VMEM((2, max(neigh, SPAN), DH), F32),
+            pltpu.VMEM((blocks, nbt, 2, g, DH), BF16),
+            pltpu.VMEM((2, n_tp, SPAN, width), BF16),
+            pltpu.VMEM((units, 2, g, DH), BF16),
+            pltpu.VMEM((2, g, DH), F32),
+            pltpu.VMEM((2, units, SPAN, wide), BF16),
             pltpu.VMEM(kv_shape, BF16),
             pltpu.VMEM(kv_shape, BF16),
             pltpu.VMEM(kv_shape, BF16),
@@ -374,15 +459,23 @@
             pltpu.VMEM((units, SPAN, DH), F32),
             pltpu.VMEM((units, SPAN, DH), F32),
             pltpu.VMEM((units, NBR - 1, SPAN, DH), F32),
-            pltpu.VMEM((2, units, PAD, wide), BF16),
+            pltpu.VMEM((2, units, SPAN, wide), BF16),
+            pltpu.VMEM((2, g, DH), F32),
+            pltpu.VMEM((units, 2, g, DH), BF16),
             pltpu.VMEM((2, NBR, blocks, SPAN, width), BF16),
-            pltpu.VMEM((2, NBR, blocks, TAIL, width), BF16),
-            dma((2, n_tp, nbt, 2)),
-            dma((2, units, 2)),
+            pltpu.VMEM((NBR, blocks, nbt, 2, g, DH), BF16),
+            dma((2, n_tp)),
+            dma((2, n_tp)),
+            dma((2, n_tp)),
+            dma((2, n_tp, nbt)),
+            dma((2, units)),
+            dma((n_tp, nbt)),
+            dma((units,)),
             dma((units, NBR - 1)),
             dma((units, NBR - 1)),
             dma((2, units, 2)),
             dma((2, NBR, blocks, nbt, 2)),
+            dma((3,)),
             dma((2, n_ctx)),
             dma((2, n_ctx, nbc)),
         ],
@@ -395,8 +488,7 @@
         cotangent[0],
         keys.reshape(kv_shape),
         values.reshape(kv_shape),
-        jnp.asarray(cosine),
-        jnp.asarray(sine),
+        jnp.asarray(np.stack([cosine, sine])),
     )
     return (att[None], gq[None], gk.reshape(keys.shape), gv.reshape(values.shape))
 

time: 109 us -> 89.6 us (0.82)
  Pallas kernels: 97.4 us -> 79.3 us
    pallas_call x1, Pallas kernels: 97.4 us -> 79.3 us  [shards(): pl.pallas_call(functools.partial(kernel, n_ctx, n_tp, blocks, hc, ht), ou...]
    unnamed x18 -> x16, local copies, waits for them, and re-layouts: 10 us -> 9.27 us
where the time goes in v2:
time: 89.6 us; the launch traced here: 89.3 us
  Pallas kernels  79.3 us (89%)
  local copies, waits for them, and re-layouts  9.36 us (10%)
    pallas_call x1, Pallas kernels, shards(): pl.pallas_call(functools.partial(kernel, n_ctx, n_tp, blocks, hc, ht), ou...  79.3 us
    unnamed x16, local copies, waits for them, and re-layouts  9.27 us

profile of v2, /device:TPU:24, one launch (start us, length us, event | category | flops | bytes accessed | tf_op | source)
XLA Modules:
  0.0 89.3 jit_solution(13426389794219310712)
XLA Ops:
  0.6 0.0 copy-start.5
  0.6 0.7 copy-done.5
  1.3 0.1 copy.10.lengths
  1.4 0.0 copy-start
  1.4 1.2 %copy-done = bf16[1,2,1,16,128,128]{5,4,3,2,1,0:T(8,128)(2,1)S(1)} copy-done((bf16[1,2,1,16,128,128]{5,4,3,2,1,0:T(8,128)(2,1)S(1)}, bf16[1,2,1,16,128,128]{5,4,3,2,1,0:T(8,128)(2,1)}, u32[]{:S(2)}) %copy-start) | copy-done | bytes 1048600
  2.6 0.0 copy-start.1
  2.6 1.2 %copy-done.1 = bf16[1,2,1,16,128,128]{5,4,3,2,1,0:T(8,128)(2,1)S(1)} copy-done((bf16[1,2,1,16,128,128]{5,4,3,2,1,0:T(8,128)(2,1)S(1)}, bf16[1,2,1,16,128,128]{5,4,3,2,1,0:T(8,128)(2,1)}, u32[]{:S(2)}) %copy-start.1) | copy-done | bytes 1048600
  3.9 0.0 copy-start.2
  3.9 0.9 %copy-done.2 = bf16[1,128,1024]{2,1,0:T(8,128)(2,1)S(1)} copy-done((bf16[1,128,1024]{2,1,0:T(8,128)(2,1)S(1)}, bf16[1,128,1024]{2,1,0:T(8,128)(2,1)}, u32[]{:S(2)}) %copy-start.2) | copy-done | bytes 262168
  4.8 0.0 copy-start.3
  4.8 0.9 %copy-done.3 = bf16[1,128,1024]{2,1,0:T(8,128)(2,1)S(1)} copy-done((bf16[1,128,1024]{2,1,0:T(8,128)(2,1)S(1)}, bf16[1,128,1024]{2,1,0:T(8,128)(2,1)}, u32[]{:S(2)}) %copy-start.3) | copy-done | bytes 262168
  5.8 0.0 copy-start.4
  5.8 0.9 %copy-done.4 = f32[2,128,128]{2,1,0:T(8,128)S(1)} copy-done((f32[2,128,128]{2,1,0:T(8,128)S(1)}, f32[2,128,128]{2,1,0:T(8,128)}, u32[]{:S(2)}) %copy-start.4) | copy-done | bytes 131096
  6.7 79.3 %shard_map.93 = (bf16[128,1024]{1,0:T(8,128)(2,1)S(1)}, bf16[128,1024]{1,0:T(8,128)(2,1)S(1)}, bf16[2,16,128,128]{3,2,1,0:T(8,128)(2,1)S(1)}, bf16[2,16,128,128]{3,2,1,0:T(8,128)(2,1)S(1)}) custom-call(s32[4,2]{1,0:T(4,128)S(1)} %copy.10.lengths, bf16[128,1024]{1,0:T(8,128)(2,1)S(1)} %bitcast.17, bf16[128,1024]{1,0:T(8,128)(2,1)S(1)} %bitcast.18, ...), custom_call_target="tpu_custom_call" | custom-call | tf_op jit(solution)/shard_map/pallas_call | solution.py:432
  86.0 0.7 copy.17
  86.7 0.7 copy.18
  87.4 1.0 %copy.19 = bf16[1,2,1,16,128,128]{5,4,3,2,1,0:T(8,128)(2,1)} copy(bf16[1,2,1,16,128,128]{5,4,3,2,1,0:T(8,128)(2,1)S(1)} %bitcast.16) | data formatting | bytes 2097152
  88.4 1.0 %copy.20 = bf16[1,2,1,16,128,128]{5,4,3,2,1,0:T(8,128)(2,1)} copy(bf16[1,2,1,16,128,128]{5,4,3,2,1,0:T(8,128)(2,1)S(1)} %bitcast.15) | data formatting | bytes 2097152
Async XLA Ops:
  0.6 0.7 copy-start.5
  1.4 1.2 %copy-start = (bf16[1,2,1,16,128,128]{5,4,3,2,1,0:T(8,128)(2,1)S(1)}, bf16[1,2,1,16,128,128]{5,4,3,2,1,0:T(8,128)(2,1)}, u32[]{:S(2)}) copy-start(bf16[1,2,1,16,128,128]{5,4,3,2,1,0:T(8,128)(2,1)} %param.7) | copy-start | bytes 3145732
  2.6 1.2 %copy-start.1 = (bf16[1,2,1,16,128,128]{5,4,3,2,1,0:T(8,128)(2,1)S(1)}, bf16[1,2,1,16,128,128]{5,4,3,2,1,0:T(8,128)(2,1)}, u32[]{:S(2)}) copy-start(bf16[1,2,1,16,128,128]{5,4,3,2,1,0:T(8,128)(2,1)} %param.8) | copy-start | bytes 3145732
  3.9 0.9 %copy-start.2 = (bf16[1,128,1024]{2,1,0:T(8,128)(2,1)S(1)}, bf16[1,128,1024]{2,1,0:T(8,128)(2,1)}, u32[]{:S(2)}) copy-start(bf16[1,128,1024]{2,1,0:T(8,128)(2,1)} %param.6) | copy-start | bytes 786436
  4.8 0.9 %copy-start.3 = (bf16[1,128,1024]{2,1,0:T(8,128)(2,1)S(1)}, bf16[1,128,1024]{2,1,0:T(8,128)(2,1)}, u32[]{:S(2)}) copy-start(bf16[1,128,1024]{2,1,0:T(8,128)(2,1)} %param.9) | copy-start | bytes 786436
  5.8 0.9 %copy-start.4 = (f32[2,128,128]{2,1,0:T(8,128)S(1)}, f32[2,128,128]{2,1,0:T(8,128)}, u32[]{:S(2)}) copy-start(f32[2,128,128]{2,1,0:T(8,128)} %constant.2.clone.tables_in) | copy-start | bytes 393220

commit v3 on v2

--- a/solution.py
+++ b/solution.py
@@ -37,8 +37,8 @@
     lengths, queries, cotangent, keys, values, tables_in,
     att_out, gq_out, gk_out, gv_out,
     tokens, tables, firsts, stage, rfirst, ffirst, rin, kbuf, vbuf, gkbuf, gvbuf, qw, gw, ebuf, pbuf, dpbuf,
-    mtile, stat, pstat, sback, fback, tback, bmain, btail,
-    z_send, z_recv, relay_send, x_send, x_recv, f_send, f_recv, st_send, st_recv, bk_send, bk_recv,
+    mtile, stat, pstat, sback, fback, tback, bstage, bmain, btail,
+    z_send, z_recv, relay_send, x_send, x_recv, f_send, f_recv, st_send, st_recv, bk_send, bk_recv, bx_recv, bf_send,
     tok_sem, kv_sem, out_sem,
 ):
     g = min(hc, ht)
@@ -201,7 +201,7 @@
         return x * cos_ref[:rows] + (turned if sign > 0 else -turned)
 
     def order(k):
-        return (me_c + k) % n_ctx
+        return (jnp.where(w == blocks - 1, 0, me_c) + k) % n_ctx
 
     @pl.loop(0, n_ctx)
     def _(k):
@@ -307,11 +307,27 @@
         for a in range(2):
             act(
                 sback.at[a, unit], bmain.at[a, n, j, :, columns], bk_send.at[a, unit, 0],
-                bk_recv.at[a, n, j, kb, 0], jnp.minimum(to, n_ctx - 1), t, to < n_ctx,
+                bk_recv.at[a, n, j, kb, 0], me_c, t, to == me_c,
+            )
+            act(
+                sback.at[a, unit], bstage.at[a, t, :, columns], bk_send.at[a, unit, 0],
+                bx_recv.at[a, t, kb], jnp.minimum(to, n_ctx - 1), me_t,
+                jnp.logical_and(to < n_ctx, to != me_c),
             )
         act(
             tback.at[unit], btail.at[n, w, kb], bk_send.at[0, unit, 1], bk_recv.at[0, n, w, kb, 1], c, t, True
         )
+
+    def back_forward(tq, act):
+        j = jnp.where(w == blocks - 1, 0, w + 1)
+        for kb in range(nbt):
+            columns = pl.ds(kb * wide, wide)
+            ok = jnp.logical_and(used(w), head_block(tq, kb)[0] != me_c)
+            for a in range(2):
+                act(
+                    bstage.at[a, tq, :, columns], bmain.at[a, n, j, :, columns], bf_send.at[a, tq, kb],
+                    bk_recv.at[a, n, j, kb, 0], me_c, tq, ok,
+                )
 
     def out_copies(c, sb):
         heads = pl.ds(sb * g, g)
@@ -361,6 +377,17 @@
         for copy in out_copies(c, sb):
             copy.start()
 
+    for tq in range(n_tp):
+        for kb in range(nbt):
+            ok = jnp.logical_and(used(w), head_block(tq, kb)[0] != me_c)
+
+            @pl.when(ok)
+            def _():
+                for a in range(2):
+                    arrive(bstage.at[a, tq, :, pl.ds(kb * wide, wide)], bx_recv.at[a, tq, kb])
+
+        back_forward(tq, start)
+
     shifted_cos = pltpu.roll(cos_ref[:SPAN], SPAN - 1, 0)
     shifted_sin = pltpu.roll(sin_ref[:SPAN], SPAN - 1, 0)
     for j in range(blocks):
@@ -397,6 +424,8 @@
 
     z_sends(sent)
     f_sends(sent)
+    for tq in range(n_tp):
+        back_forward(tq, sent)
     for tq in range(n_tp):
         for a in range(2):
             x_sends(tq, a, sent, used(w))
@@ -462,6 +491,7 @@
             pltpu.VMEM((2, units, SPAN, wide), BF16),
             pltpu.VMEM((2, g, DH), F32),
             pltpu.VMEM((units, 2, g, DH), BF16),
+            pltpu.VMEM((2, n_tp, SPAN, width), BF16),
             pltpu.VMEM((2, NBR, blocks, SPAN, width), BF16),
             pltpu.VMEM((NBR, blocks, nbt, 2, g, DH), BF16),
             dma((2, n_tp)),
@@ -475,6 +505,8 @@
             dma((units, NBR - 1)),
             dma((2, units, 2)),
             dma((2, NBR, blocks, nbt, 2)),
+            dma((2, n_tp, nbt)),
+            dma((2, n_tp, nbt)),
             dma((3,)),
             dma((2, n_ctx)),
             dma((2, n_ctx, nbc)),

time: 89.6 us -> 75 us (0.84)
  the two profiles are of different devices: /device:TPU:24 before, /device:TPU:10 now
where the time goes in v3:
time: 75 us; the launch traced here: 74.7 us
  Pallas kernels  64.7 us (86%)
  local copies, waits for them, and re-layouts  9.36 us (12%)
    pallas_call x1, Pallas kernels, shards(): pl.pallas_call(functools.partial(kernel, n_ctx, n_tp, blocks, hc, ht), ou...  64.7 us
    unnamed x16, local copies, waits for them, and re-layouts  9.27 us

profile of v3, /device:TPU:10, one launch (start us, length us, event | category | flops | bytes accessed | tf_op | source)
XLA Modules:
  0.0 74.7 jit_solution(2853703228561827285)
XLA Ops:
  0.6 0.0 copy-start.5
  0.6 0.7 copy-done.5
  1.3 0.1 copy.10.lengths
  1.4 0.0 copy-start
  1.4 1.2 %copy-done = bf16[1,2,1,16,128,128]{5,4,3,2,1,0:T(8,128)(2,1)S(1)} copy-done((bf16[1,2,1,16,128,128]{5,4,3,2,1,0:T(8,128)(2,1)S(1)}, bf16[1,2,1,16,128,128]{5,4,3,2,1,0:T(8,128)(2,1)}, u32[]{:S(2)}) %copy-start) | copy-done | bytes 1048600
  2.6 0.0 copy-start.1
  2.6 1.2 %copy-done.1 = bf16[1,2,1,16,128,128]{5,4,3,2,1,0:T(8,128)(2,1)S(1)} copy-done((bf16[1,2,1,16,128,128]{5,4,3,2,1,0:T(8,128)(2,1)S(1)}, bf16[1,2,1,16,128,128]{5,4,3,2,1,0:T(8,128)(2,1)}, u32[]{:S(2)}) %copy-start.1) | copy-done | bytes 1048600
  3.9 0.0 copy-start.2
  3.9 0.9 %copy-done.2 = bf16[1,128,1024]{2,1,0:T(8,128)(2,1)S(1)} copy-done((bf16[1,128,1024]{2,1,0:T(8,128)(2,1)S(1)}, bf16[1,128,1024]{2,1,0:T(8,128)(2,1)}, u32[]{:S(2)}) %copy-start.2) | copy-done | bytes 262168
  4.8 0.0 copy-start.3
  4.8 0.9 %copy-done.3 = bf16[1,128,1024]{2,1,0:T(8,128)(2,1)S(1)} copy-done((bf16[1,128,1024]{2,1,0:T(8,128)(2,1)S(1)}, bf16[1,128,1024]{2,1,0:T(8,128)(2,1)}, u32[]{:S(2)}) %copy-start.3) | copy-done | bytes 262168
  5.8 0.0 copy-start.4
  5.8 0.9 %copy-done.4 = f32[2,128,128]{2,1,0:T(8,128)S(1)} copy-done((f32[2,128,128]{2,1,0:T(8,128)S(1)}, f32[2,128,128]{2,1,0:T(8,128)}, u32[]{:S(2)}) %copy-start.4) | copy-done | bytes 131096
  6.7 64.7 %shard_map.93 = (bf16[128,1024]{1,0:T(8,128)(2,1)S(1)}, bf16[128,1024]{1,0:T(8,128)(2,1)S(1)}, bf16[2,16,128,128]{3,2,1,0:T(8,128)(2,1)S(1)}, bf16[2,16,128,128]{3,2,1,0:T(8,128)(2,1)S(1)}) custom-call(s32[4,2]{1,0:T(4,128)S(1)} %copy.10.lengths, bf16[128,1024]{1,0:T(8,128)(2,1)S(1)} %bitcast.17, bf16[128,1024]{1,0:T(8,128)(2,1)S(1)} %bitcast.18, ...), custom_call_target="tpu_custom_call" | custom-call | tf_op jit(solution)/shard_map/pallas_call | solution.py:461
  71.3 0.7 copy.17
  72.0 0.7 copy.18
  72.7 1.0 %copy.19 = bf16[1,2,1,16,128,128]{5,4,3,2,1,0:T(8,128)(2,1)} copy(bf16[1,2,1,16,128,128]{5,4,3,2,1,0:T(8,128)(2,1)S(1)} %bitcast.16) | data formatting | bytes 2097152
  73.7 1.0 %copy.20 = bf16[1,2,1,16,128,128]{5,4,3,2,1,0:T(8,128)(2,1)} copy(bf16[1,2,1,16,128,128]{5,4,3,2,1,0:T(8,128)(2,1)S(1)} %bitcast.15) | data formatting | bytes 2097152
Async XLA Ops:
  0.6 0.7 copy-start.5
  1.4 1.2 %copy-start = (bf16[1,2,1,16,128,128]{5,4,3,2,1,0:T(8,128)(2,1)S(1)}, bf16[1,2,1,16,128,128]{5,4,3,2,1,0:T(8,128)(2,1)}, u32[]{:S(2)}) copy-start(bf16[1,2,1,16,128,128]{5,4,3,2,1,0:T(8,128)(2,1)} %param.7) | copy-start | bytes 3145732
  2.6 1.2 %copy-start.1 = (bf16[1,2,1,16,128,128]{5,4,3,2,1,0:T(8,128)(2,1)S(1)}, bf16[1,2,1,16,128,128]{5,4,3,2,1,0:T(8,128)(2,1)}, u32[]{:S(2)}) copy-start(bf16[1,2,1,16,128,128]{5,4,3,2,1,0:T(8,128)(2,1)} %param.8) | copy-start | bytes 3145732
  3.9 0.9 %copy-start.2 = (bf16[1,128,1024]{2,1,0:T(8,128)(2,1)S(1)}, bf16[1,128,1024]{2,1,0:T(8,128)(2,1)}, u32[]{:S(2)}) copy-start(bf16[1,128,1024]{2,1,0:T(8,128)(2,1)} %param.6) | copy-start | bytes 786436
  4.8 0.9 %copy-start.3 = (bf16[1,128,1024]{2,1,0:T(8,128)(2,1)S(1)}, bf16[1,128,1024]{2,1,0:T(8,128)(2,1)}, u32[]{:S(2)}) copy-start(bf16[1,128,1024]{2,1,0:T(8,128)(2,1)} %param.9) | copy-start | bytes 786436
  5.8 0.9 %copy-start.4 = (f32[2,128,128]{2,1,0:T(8,128)S(1)}, f32[2,128,128]{2,1,0:T(8,128)}, u32[]{:S(2)}) copy-start(f32[2,128,128]{2,1,0:T(8,128)} %constant.2.clone.tables_in) | copy-start | bytes 393220

commit v4 on v3

--- a/solution.py
+++ b/solution.py
@@ -512,7 +512,7 @@
             dma((2, n_ctx, nbc)),
         ],
         compiler_params=pltpu.CompilerParams(
-            collective_id=0, has_side_effects=True, vmem_limit_bytes=48 * 1024 * 1024
+            collective_id=0, has_side_effects=True, vmem_limit_bytes=61 * 1024 * 1024
         ),
     )(
         lengths[0].reshape(-1, NBR),

time: 75 us -> 73.5 us (0.980)
  local copies, waits for them, and re-layouts: 9.36 us -> 7.34 us
    unnamed x16 -> x10, local copies, waits for them, and re-layouts: 9.27 us -> 6.67 us
where the time goes in v4:
time: 73.5 us; the launch traced here: 73.2 us
  Pallas kernels  65.2 us (89%)
  local copies, waits for them, and re-layouts  7.34 us (10%)
    pallas_call x1, Pallas kernels, shards(): pl.pallas_call(functools.partial(kernel, n_ctx, n_tp, blocks, hc, ht), ou...  65.2 us
    unnamed x10, local copies, waits for them, and re-layouts  6.67 us

profile of v4, /device:TPU:10, one launch (start us, length us, event | category | flops | bytes accessed | tf_op | source)
XLA Modules:
  0.0 73.2 jit_solution(9656981800637760846)
XLA Ops:
  0.6 0.0 copy-start.2
  0.6 0.7 copy-done.2
  1.3 0.7 copy.10.lengths
  2.0 65.2 %shard_map.93 = (bf16[128,1024]{1,0:T(8,128)(2,1)}, bf16[128,1024]{1,0:T(8,128)(2,1)}, bf16[2,16,128,128]{3,2,1,0:T(8,128)(2,1)}, bf16[2,16,128,128]{3,2,1,0:T(8,128)(2,1)}) custom-call(s32[4,2]{1,0:T(4,128)} %copy.10.lengths, bf16[128,1024]{1,0:T(8,128)(2,1)} %bitcast.17, bf16[128,1024]{1,0:T(8,128)(2,1)} %bitcast.18, bf16[2,16,128,128]{3,2,1,0:T(8,128)(2,1)} %bitcast.13, ...), custom_call_target="tpu_custom_call" | custom-call | tf_op jit(solution)/shard_map/pallas_call | solution.py:461
  67.2 0.0 copy-start.1
  67.2 1.8 %copy.17 = bf16[1,128,1024]{2,1,0:T(8,128)(2,1)} copy(bf16[1,128,1024]{2,1,0:T(8,128)(2,1)} %bitcast.20) | data formatting | bytes 524288
  69.0 1.7 %copy.18 = bf16[1,128,1024]{2,1,0:T(8,128)(2,1)} copy(bf16[1,128,1024]{2,1,0:T(8,128)(2,1)} %bitcast.19) | data formatting | bytes 524288
  70.7 0.0 copy-done.1
  70.7 0.0 copy-start
  70.7 1.0 %copy.19 = bf16[1,2,1,16,128,128]{5,4,3,2,1,0:T(8,128)(2,1)} copy(bf16[1,2,1,16,128,128]{5,4,3,2,1,0:T(8,128)(2,1)S(1)} %bitcast.16) | data formatting | bytes 2097152
  71.6 0.6 copy-done
  72.3 1.0 %copy.20 = bf16[1,2,1,16,128,128]{5,4,3,2,1,0:T(8,128)(2,1)} copy(bf16[1,2,1,16,128,128]{5,4,3,2,1,0:T(8,128)(2,1)S(1)} %bitcast.15) | data formatting | bytes 2097152
Async XLA Ops:
  0.6 0.7 copy-start.2
  67.2 3.4 %copy-start.1 = (bf16[2,16,128,128]{3,2,1,0:T(8,128)(2,1)S(1)}, bf16[2,16,128,128]{3,2,1,0:T(8,128)(2,1)}, u32[]{:S(2)}) copy-start(bf16[2,16,128,128]{3,2,1,0:T(8,128)(2,1)} %get-tuple-element.10) | copy-start | bytes 3145732
  70.7 1.6 %copy-start = (bf16[2,16,128,128]{3,2,1,0:T(8,128)(2,1)S(1)}, bf16[2,16,128,128]{3,2,1,0:T(8,128)(2,1)}, u32[]{:S(2)}) copy-start(bf16[2,16,128,128]{3,2,1,0:T(8,128)(2,1)} %get-tuple-element.11) | copy-start | bytes 3145732
